TPU v7x, 256 devices: a whole 4x4x8 slice. The times are simulated.
256 devices in a mesh: row: 16 (over y, x), col: 16 (over z, core).
Axes of the slice: x: 4, y: 4, z: 8, core: 2. Of those that a mesh axis runs over, the one named last changes fastest.
Arguments:
- eigenbasis: bfloat16 [16384, 16384], P('row', 'col'), may hold values from -0.046875 to 0.046875
- gradient: float32 [16384, 2048], P('row', 'col'), may hold values from -6 to 6
- moment_one: float32 [16384, 2048], P('col', 'row'), may hold values from -0.6 to 0.6
- moment_two: float32 [16384, 2048], P('col', 'row'), may hold values from 0.0001 to 0.01
Outputs:
- update: float32 [16384, 2048], P('row', 'col')
- new_one: float32 [16384, 2048], P('col', 'row')
- new_two: float32 [16384, 2048], P('col', 'row')
All inputs are finite; a program needn't handle non-finite values.
Results may differ from a plain program's by a relative error of at most 0.004.
Values may be sent and summed in bfloat16 or wider, within the bound.
No kernel may reach another device: no remote copies, remote signals or barrier semaphores. Data moves between devices by JAX's collectives and lax.ppermute only.
A program may use at most 64 MiB of HBM per device.

v0:
```python
import jax
import jax.numpy as jnp
from jax import lax
from jax.sharding import PartitionSpec as P

beta_one = 0.9
beta_two = 0.999
step_count = 10
epsilon = 1e-08


def copy_for_each(shard, axis):
    count = lax.axis_size(axis)
    return lax.all_to_all(
        jnp.broadcast_to(shard[None], (count, *shard.shape)), axis, 0, 0, tiled=True
    )


def joined_along(blocks, dim):
    lengths = list(blocks.shape[1:])
    lengths[dim] *= blocks.shape[0]
    return jnp.moveaxis(blocks, 0, dim).reshape(lengths)


def gather_directly(shard, axis, dim):
    blocks = copy_for_each(shard, axis)
    return joined_along(blocks, dim)


def local(eigenbasis, gradient, moment_one, moment_two):
    grad_half = gradient.astype(jnp.bfloat16)
    whole_grad = lax.all_gather(grad_half, "col", axis=1, tiled=True)
    segment = whole_grad
    rotated = lax.psum_scatter(
        lax.dot_general(
            segment, eigenbasis, (((0,), (0,)), ((), ())), preferred_element_type=jnp.float32
        ),
        "row",
        scatter_dimension=0,
        tiled=True,
    ).T
    new_one = beta_one * moment_one + (1.0 - beta_one) * rotated
    new_two = beta_two * moment_two + (1.0 - beta_two) * rotated * rotated
    corr_one = 1.0 - beta_one**step_count
    corr_two = 1.0 - beta_two**step_count
    direction = (new_one / corr_one / (jnp.sqrt(new_two / corr_two) + epsilon)).astype(jnp.bfloat16)
    whole_dir = gather_directly(direction, "row", 1)
    segment = whole_dir
    update = lax.psum_scatter(
        lax.dot_general(
            segment, eigenbasis, (((0,), (1,)), ((), ())), preferred_element_type=jnp.float32
        ),
        "col",
        scatter_dimension=0,
        tiled=True,
    ).T
    return (update, new_one, new_two)


def solution(mesh):
    placed = (P("row", "col"), P("row", "col"), P("col", "row"), P("col", "row"))
    return jax.shard_map(
        local,
        mesh=mesh,
        in_specs=placed,
        out_specs=(P("row", "col"), P("col", "row"), P("col", "row")),
        check_vma=False,
    )
```

profile of v0, /device:TPU:6, one launch (start us, length us, event | category | flops | bytes accessed | tf_op | source)
XLA Modules:
  0.0 303.5 jit_solution(15810952796670115565)
XLA Ops:
  7.2 0.0 copy-start
  7.2 0.0 all-gather.2.cloned.1.call-start
  7.2 1.9 convert_element_type.6
  9.1 0.0 all-gather.2.cloned.1.call-update
  9.2 0.0 reduce-scatter.3.cloned.1.call-start
  9.2 53.0 %all-gather.2.cloned.1.call-done = bf16[1024,2048]{1,0:T(8,128)(2,1)} async-done(((bf16[1024,128]{1,0:T(8,128)(2,1)}), bf16[1024,2048]{1,0:T(8,128)(2,1)}) %all-gather.2.cloned.1.call-update) | async-done | bytes 4194320 | tf_op jit(solution)/shard_map/all_gather | solution.py:32
  62.2 0.0 copy-done
  62.2 9.1 %fusion.4 = f32[2048,1024]{1,0:T(8,128)} fusion(bf16[1024,2048]{1,0:T(8,128)(2,1)} %all-gather.2.cloned.1.call-done, bf16[1024,1024]{1,0:T(8,128)(2,1)S(1)} %copy-done), kind=kOutput, calls=%fused_computation.5 | convolution fusion | flops 4294967296 | bytes 14680064 | tf_op jit(solution)/shard_map/dot_general | solution.py:35
  71.3 0.0 copy-start.1
  71.3 0.0 copy-start.2
  71.3 0.0 reduce-scatter.3.cloned.1.call-update
  71.4 0.0 reduce-scatter.5.cloned.1.call-start
  71.4 1.0 copy-done.1
  72.4 1.0 copy.13
  73.4 0.0 copy-done.2
  73.4 1.0 copy.14
  74.4 86.4 %reduce-scatter.3.cloned.1.call-done = f32[128,1024]{1,0:T(8,128)} async-done(((f32[2048,1024]{1,0:T(8,128)}), f32[128,1024]{1,0:T(8,128)}) %reduce-scatter.3.cloned.1.call-update) | async-done | bytes 524304 | tf_op jit(solution)/shard_map/reduce_scatter | solution.py:34
  160.8 1.7 divide_convert_fusion
  162.5 0.5 broadcast_in_dim.2
  163.0 53.5 %all_to_all.5 = bf16[16,1024,128]{1,2,0:T(8,128)(2,1)S(1)} all-to-all(bf16[16,1024,128]{1,2,0:T(8,128)(2,1)S(1)} %broadcast_in_dim.2), channel_id=1, replica_groups=mesh['row'=16,'col'=16] {'row'}, dimensions={0} | all-to-all | bytes 8388608 | tf_op jit(solution)/shard_map/all_to_all | solution.py:14
  216.5 7.1 %fusion.5 = f32[2048,1024]{1,0:T(8,128)} fusion(bf16[1024,2048]{0,1:T(8,128)(2,1)S(1)} %bitcast.15, bf16[1024,1024]{1,0:T(8,128)(2,1)S(1)} %copy-done), kind=kOutput, calls=%fused_computation.6 | convolution fusion | flops 4294967296 | bytes 14680064 | tf_op jit(solution)/shard_map/dot_general | solution.py:50
  223.6 0.0 reduce-scatter.5.cloned.1.call-update
  223.6 1.0 copy.16
  224.6 1.0 copy.17
  225.6 69.3 %reduce-scatter.5.cloned.1.call-done = f32[128,1024]{1,0:T(8,128)} async-done(((f32[2048,1024]{1,0:T(8,128)}), f32[128,1024]{1,0:T(8,128)}) %reduce-scatter.5.cloned.1.call-update) | async-done | bytes 524304 | tf_op jit(solution)/shard_map/reduce_scatter | solution.py:49
  294.9 2.0 copy.15
Async XLA Ops:
  7.2 55.1 %copy-start = (bf16[1024,1024]{1,0:T(8,128)(2,1)S(1)}, bf16[1024,1024]{1,0:T(8,128)(2,1)}, u32[]{:S(2)}) copy-start(bf16[1024,1024]{1,0:T(8,128)(2,1)} %param.4) | copy-start | bytes 6291460
  7.2 55.1 %all-gather.2.cloned.1.call-start = ((), (), s32[]{:S(2)}) async-start(), calls=%async_computation.3 | async-start | bytes 4456448 | tf_op jit(solution)/shard_map/all_gather | solution.py:32
  9.2 151.6 %reduce-scatter.3.cloned.1.call-start = ((), (), s32[]{:S(2)}) async-start(), calls=%async_computation.4 | async-start | bytes 8912896 | tf_op jit(solution)/shard_map/reduce_scatter | solution.py:34
  71.3 1.0 copy-start.1
  71.3 2.0 copy-start.2
  71.4 223.6 %reduce-scatter.5.cloned.1.call-start = ((), (), s32[]{:S(2)}) async-start(), calls=%async_computation.5 | async-start | bytes 8912896 | tf_op jit(solution)/shard_map/reduce_scatter | solution.py:49
Sparse Core Ops, SparseCore 0:
  10.3 51.8 all-gather.1
  71.5 89.2 reduce-scatter.2
  223.7 71.1 reduce-scatter.4
where the time goes:
time: 304 us; the launch traced here: 303 us
  waiting for transfers between devices  209 us (69%)
  blocking collectives  53.5 us (18%)
  matrix products  16.2 us (5%)
  between operations  13.8 us (5%)
  local copies, waits for them, and re-layouts  7.51 us (2%)
  other arithmetic  3.62 us (1%)
    reduce_scatter x1, waiting for transfers between devices, local(): lax.psum_scatter(lax.dot_general(segment, eigenbasis, (((0,), (0,)), ((),...  86.4 us
    reduce_scatter x1, waiting for transfers between devices, local(): lax.psum_scatter(lax.dot_general(segment, eigenbasis, (((0,), (1,)), ((),...  69.3 us
    all_to_all x1, blocking collectives, copy_for_each(): lax.all_to_all(jnp.broadcast_to(shard[None], (count, *shard.shape)), axis...  53.5 us
    all_gather x1, waiting for transfers between devices, local(): whole_grad = lax.all_gather(grad_half, 'col', axis=1, tiled=True)  53 us
    dot_general x1, matrix products, local(): lax.dot_general(segment, eigenbasis, (((0,), (0,)), ((), ())), preferred_...  9.08 us
    dot_general x1, matrix products, local(): lax.dot_general(segment, eigenbasis, (((0,), (1,)), ((), ())), preferred_...  7.13 us
    unnamed x11, local copies, waits for them, and re-layouts  6.99 us
  transfers between devices with their start and end apart: 3, of which 3 were waited for; matrix products, arithmetic and copies ran while one was open for 1% of the time, Pallas kernels for 0%

commit v1 on v0

v1 whole, which is shorter than its diff:
```python
import jax
import jax.numpy as jnp
from jax import lax
from jax.experimental import pallas as pl
from jax.experimental.pallas import tpu as pltpu
from jax.sharding import Mesh, PartitionSpec as P


beta_one = 0.9
beta_two = 0.999
step_count = 10
epsilon = 1e-08

CHUNKS = 2
ROWS = 32
HALF = 64
TILE = 256
AXES = ("y", "x", "z", "core")
f32 = jnp.float32
bf16 = jnp.bfloat16


def permute(value, to):
    pairs = []
    for i in range(256):
        y, x, z, c = i // 64, i // 16 % 4, i // 2 % 8, i % 2
        y, x, z, c = to(y, x, z, c)
        pairs.append((i, ((y % 4 * 4 + x % 4) * 8 + z % 8) * 2 + c))
    return lax.ppermute(value, AXES, pairs)


def swap(value):
    return permute(value, lambda y, x, z, c: (y, x, z, 1 - c))


def up(value):
    return permute(value, lambda y, x, z, c: (y, x, z + 1, c))


def down(value):
    return permute(value, lambda y, x, z, c: (y, x, z - 1, c))


def across(value, stage, d, flip):
    return permute(value, lambda y, x, z, c: (y, x + d, z, c) if c ^ flip == stage else (y + d, x, z, c))


def where_am_i():
    return tuple(lax.axis_index(a) for a in AXES)


def table_one(flip):
    y, x, z, core = where_am_i()
    offset = jnp.array([0, -1, -2, -3, 1, 2, 3, 4], jnp.int32)
    b = 2 * ((z + offset[:, None] + 16) % 8) + jnp.arange(2, dtype=jnp.int32)[None]
    by, bx = b // 4, b % 4
    place = jnp.where(core == flip, 4 * ((bx - x + 4) % 4) + by, 4 * ((by - y + 4) % 4) + bx)
    return place.reshape(16).astype(jnp.int32)


def table_two(flip):
    y, x, z, core = where_am_i()
    u = jnp.arange(16, dtype=jnp.int32)
    d2, d1 = u // 4, u % 4
    dx, dy = jnp.where(core == flip, d1, d2), jnp.where(core == flip, d2, d1)
    b = 4 * ((y - dy + 4) % 4) + (x - dx + 4) % 4
    return (2 * ((b // 2 - z + 8) % 8) + b % 2).astype(jnp.int32)


def call(kernel, table, operands, outs, scratch, flops):
    size = sum(a.size * a.dtype.itemsize for a in (*operands, *outs))
    return pl.pallas_call(
        kernel,
        out_shape=outs,
        in_specs=[pl.BlockSpec(memory_space=pltpu.SMEM)]
        + [pl.BlockSpec(memory_space=pltpu.VMEM)] * len(operands),
        out_specs=[pl.BlockSpec(memory_space=pltpu.VMEM)] * len(outs),
        scratch_shapes=scratch,
        cost_estimate=pl.CostEstimate(flops=flops, bytes_accessed=size, transcendentals=0),
        compiler_params=pltpu.CompilerParams(vmem_limit_bytes=24 * 2**20),
    )(table, *operands)


def forward_kernel(chunk):
    def kernel(table, *refs):
        pieces, (near, far, o2, o1, o3, o0, lhs) = refs[:8], refs[8:]
        for c in range(2):
            for piece, ref in enumerate(pieces):
                first = ROWS * chunk if piece < 7 else 0
                lhs[table[2 * piece + c]] = ref[c, first : first + ROWS]
        k = lhs.shape[2]
        for side, basis in enumerate((near, far)):

            @pl.loop(0, k // TILE)
            def _(t):
                at = pl.ds(pl.multiple_of(t * TILE, TILE), TILE)
                to = pl.ds(pl.multiple_of(side * k + t * TILE, TILE), TILE)
                part = jnp.dot(lhs[...].reshape(16 * ROWS, k), basis[:, at], preferred_element_type=f32)
                part = part.reshape(4, 4, ROWS, TILE)
                for d, out in ((2, o2), (1, o1), (3, o3), (0, o0)):
                    out[:, :, to] = part[d].astype(out.dtype)

    return kernel


def back_kernel(table, *refs):
    lines, (near, far, ends, ahead, behind, lhs) = refs[:8], refs[8:]
    for j in range(2):
        for d2, ref in enumerate(lines[4 * j : 4 * j + 4]):
            for d1 in range(4):
                lhs[table[16 * j + 4 * d2 + d1], j] = ref[d1]
    m = lhs.shape[3] // 2

    @pl.loop(0, m // TILE)
    def _(t):
        at = pl.ds(pl.multiple_of(t * TILE, TILE), TILE)
        dims = (((1,), (1,)), ((), ()))
        part = lax.dot_general(lhs[..., :m].reshape(32 * ROWS, m), near[at, :], dims, preferred_element_type=f32)
        part += lax.dot_general(lhs[..., m:].reshape(32 * ROWS, m), far[at, :], dims, preferred_element_type=f32)
        part = part.reshape(16, 2, ROWS, TILE)
        ends[0:2, :, :, at], ends[2:4, :, :, at] = part[0:2], part[8:10]
        ahead[:, :, :, at], behind[:, :, :, at] = part[2:8], part[10:16]


def sum_kernel(mine, p0, p1, p2, p3, o2, o1, o3, o0):
    @pl.loop(0, o0.shape[1] // TILE)
    def _(t):
        at = pl.ds(pl.multiple_of(t * TILE, TILE), TILE)
        for d, out in ((2, o2), (1, o1), (3, o3), (0, o0)):
            i = lax.rem(mine[0] + d, 4)
            total = p0[i, :, at].astype(f32) + p1[i, :, at].astype(f32)
            total += p2[i, :, at].astype(f32) + p3[i, :, at].astype(f32)
            out[:, at] = total.astype(out.dtype)


def adam_kernel(chunk):
    rows = slice(ROWS * chunk, ROWS * chunk + ROWS)
    corr_one = 1.0 - beta_one**step_count
    corr_two = 1.0 - beta_two**step_count

    def kernel(unused, q0, q1, q2, q3, near, other, new_near, new_other, direction):
        m = near.shape[2]
        for side, (old, new) in enumerate(((near, new_near), (other, new_other))):

            @pl.loop(0, m // TILE)
            def _(t):
                at = pl.ds(pl.multiple_of(t * TILE, TILE), TILE)
                to = pl.ds(pl.multiple_of(side * m + t * TILE, TILE), TILE)
                rotated = q0[:, to] + q1[:, to].astype(f32) + q2[:, to].astype(f32) + q3[:, to].astype(f32)
                first = beta_one * old[0, rows, at] + (1.0 - beta_one) * rotated
                second = beta_two * old[1, rows, at] + (1.0 - beta_two) * rotated * rotated
                new[0, :, at] = first
                new[1, :, at] = second
                direction[:, to] = (first / corr_one / (jnp.sqrt(second / corr_two) + epsilon)).astype(bf16)

    return kernel


def turn_in_kernel(core, one, two, mine, theirs):
    for i, ref in enumerate((one, two)):
        turned = ref[...].T
        low, high = turned[:HALF], turned[HALF:]
        mine[i] = jnp.where(core[0] == 0, low, high)
        theirs[i] = jnp.where(core[0] == 0, high, low)


def turn_kernel(core, near0, near1, given, new_one, new_two):
    for i, out in enumerate((new_one, new_two)):
        mine = jnp.concatenate([near0[i], near1[i]])
        theirs = jnp.concatenate([given[0, i], given[1, i]])
        low = core[0] == 0
        out[...] = jnp.concatenate([jnp.where(low, mine, theirs), jnp.where(low, theirs, mine)]).T


def halves(value, core, axis=0):
    cut = [lax.dynamic_slice_in_dim(value, HALF * c, HALF, axis) for c in (core, 1 - core)]
    return cut[0], cut[1]


def ordered(mine, theirs, core, axis=0):
    return jnp.where(core == 0, jnp.concatenate([mine, theirs], axis), jnp.concatenate([theirs, mine], axis))


def step(eigenbasis, gradient, moment_one, moment_two):
    y, x, _, core = where_am_i()
    S = jax.ShapeDtypeStruct
    nothing = jnp.zeros((1,), jnp.int32)
    flops = 2 * 16 * ROWS * 1024 * 2048

    mine, theirs = halves(gradient.T.astype(bf16), core)
    own = ordered(mine[None], swap(theirs)[None], core)
    ups, downs = [own], [own]
    for _ in range(3):
        ups.append(up(ups[-1]))
        downs.append(down(downs[-1]))
    far = (up(ups[3][:, :ROWS]), down(downs[3][:, ROWS:]))
    basis = (eigenbasis, swap(eigenbasis))
    which = core.astype(jnp.int32).reshape(1)
    near_m, theirs = call(
        turn_in_kernel, which, (moment_one, moment_two), (S((2, HALF, 1024), f32),) * 2, [],
        2000 * 128 * 1024,
    )
    far_m = swap(theirs)
    big, small = S((4, ROWS, 2048), bf16), S((ROWS, 2048), bf16)
    new = S((2, ROWS, 1024), f32)
    news, lines = [], []
    for j in range(CHUNKS):
        flip = j % 2
        p = dict(zip((2, 1, 3, 0), call(
            forward_kernel(j), table_one(flip), (*ups, *downs[1:], far[j], *basis),
            (big, big, big, S((4, ROWS, 2048), f32)), [pltpu.VMEM((16, ROWS, 1024), bf16)], flops,
        )))
        for d in (2, 1, 3):
            p[d] = across(p[d], 0, d, flip)
        index = jnp.where(core == flip, y, x).astype(jnp.int32).reshape(1)
        q = dict(zip((2, 1, 3, 0), call(
            sum_kernel, index, [p[d] for d in range(4)], (small, small, small, S((ROWS, 2048), f32)), [], 2000 * ROWS * 2048,
        )))
        for d in (2, 1, 3):
            q[d] = across(q[d], 1, d, flip)
        near, far_new, direction = call(
            adam_kernel(j), nothing, [*(q[d] for d in range(4)), near_m, far_m],
            (new, new, small), [], 2000 * ROWS * 2048,
        )
        news.append((near, far_new))
        line = jnp.stack([direction, *(across(direction, 0, d, flip) for d in (1, 2, 3))])
        lines += [line, *(across(line, 1, d, flip) for d in (1, 2, 3))]
    ends, ahead, behind = call(
        back_kernel, jnp.concatenate([table_two(0), table_two(1)]), (*lines, *basis),
        [S((n, 2, ROWS, 1024), f32) for n in (4, 6, 6)], [pltpu.VMEM((16, 2, ROWS, 2048), bf16)], 2 * flops,
    )

    at_up, at_down = ends[2:, 0], ends[2:, 1]
    for s in (1, 2, 3, 4):
        to_up = at_up.astype(bf16)
        to_down = at_down.astype(bf16)
        to_up, to_down = up(to_up), down(to_down)
        at_up = to_up.astype(f32)
        if s < 4:
            mine = ahead[6 - 2 * s : 8 - 2 * s]
            at_up = mine + at_up if s > 1 else mine.at[:, 0].add(at_up)
        at_down = to_down.astype(f32)
        if s < 4:
            mine = behind[2 * s - 2 : 2 * s]
            at_down = mine + at_down if s > 1 else mine.at[:, 1].add(at_down)
    total = ends[:2] + at_up + at_down
    mine = lax.dynamic_index_in_dim(total, core, 0, False).reshape(HALF, 1024)
    theirs = lax.dynamic_index_in_dim(total, 1 - core, 0, False).reshape(HALF, 1024)
    update = ordered(mine, swap(theirs), core).T

    given = swap(jnp.stack([news[0][1], news[1][1]]))
    turned = S((1024, 128), f32)
    new_one, new_two = call(
        turn_kernel, which, [news[0][0], news[1][0], given],
        (turned, turned), [], 2000 * 128 * 1024,
    )
    return update, new_one, new_two


def solution(mesh):
    fine = Mesh(mesh.devices.reshape(4, 4, 8, 2), AXES)
    row, col = ("y", "x"), ("z", "core")
    return jax.shard_map(
        step,
        mesh=fine,
        in_specs=(P(row, col), P(row, col), P(col, row), P(col, row)),
        out_specs=(P(row, col), P(col, row), P(col, row)),
        check_vma=False,
    )
```

time: 304 us -> 189 us (0.62)
  waiting for transfers between devices: 209 us -> 82.3 us
  starting transfers between devices: 0.12 us -> 66.1 us
  blocking collectives: 53.5 us -> 0 us
  Pallas kernels: 0 us -> 23.6 us
  matrix products: 16.2 us -> 0 us
  between operations: 13.8 us -> 1.12 us
  local copies, waits for them, and re-layouts: 7.51 us -> 13.7 us
    reduce_scatter x2 -> x0, waiting for transfers between devices: 156 us -> none  [the longest x1 86.4 us: local(): lax.psum_scatter(lax.dot_general(segment, eigenbasis, (((0,), (0,)), ((),...]
    ppermute x0 -> x45, waiting for transfers between devices: none -> 82.3 us  [permute(): return lax.ppermute(value, AXES, pairs)]
    ppermute x0 -> x45, starting transfers between devices: none -> 66.1 us  [permute(): return lax.ppermute(value, AXES, pairs)]
    all_to_all x1 -> x0, blocking collectives: 53.5 us -> none  [copy_for_each(): lax.all_to_all(jnp.broadcast_to(shard[None], (count, *shard.shape)), axis...]
    all_gather x1 -> x0, waiting for transfers between devices: 53 us -> none  [local(): whole_grad = lax.all_gather(grad_half, 'col', axis=1, tiled=True)]
    pallas_call x0 -> x9, Pallas kernels: none -> 23.6 us  [call(): pl.pallas_call(kernel, out_shape=outs, in_specs=[pl.BlockSpec(memory_spac...]
    dot_general x2 -> x0, matrix products: 16.2 us -> none  [the longest x1 9.08 us: local(): lax.dot_general(segment, eigenbasis, (((0,), (0,)), ((), ())), preferred_...]
    unnamed x11 -> x44, local copies, waits for them, and re-layouts: 6.99 us -> 12.3 us
  transfers between devices with their start and end apart: 3 -> 45, of which waited for: 3 -> 22; matrix products, arithmetic and copies ran while one was open for 1% -> 2% of each run, Pallas kernels for 0% -> 6%
where the time goes in v1:
time: 189 us
  waiting for transfers between devices  82.3 us (44%)
  starting transfers between devices  66.1 us (35%)
  Pallas kernels  23.6 us (12%)
  local copies, waits for them, and re-layouts  13.7 us (7%)
  other arithmetic  1.91 us (1%)
    ppermute x45, waiting for transfers between devices, permute(): return lax.ppermute(value, AXES, pairs)  82.3 us
    ppermute x45, starting transfers between devices, permute(): return lax.ppermute(value, AXES, pairs)  66.1 us
    pallas_call x9, Pallas kernels, call(): pl.pallas_call(kernel, out_shape=outs, in_specs=[pl.BlockSpec(memory_spac...  23.6 us
    unnamed x44, local copies, waits for them, and re-layouts  12.3 us
  transfers between devices with their start and end apart: 45, of which 22 were waited for; matrix products, arithmetic and copies ran while one was open for 2% of the time, Pallas kernels for 6%

profile of v1, /device:TPU:6, one launch (start us, length us, event | category | flops | bytes accessed | tf_op | source)
XLA Modules:
  0.0 188.7 jit_solution(956098528965892868)
XLA Ops:
  2.5 2.7 %collective-permute-done = bf16[64,1024]{1,0:T(8,128)(2,1)S(1)} collective-permute-done((bf16[64,1024]{1,0:T(8,128)(2,1)S(1)}, bf16[64,1024]{1,0:T(8,128)(2,1)S(1)}, u32[]{:S(2)}, u32[]{:S(2)}) %collective-permute-start) | collective-permute-done | bytes 131104 | tf_op jit(solution)/shard_map/ppermute | solution.py:29
  5.3 5.9 %collective-permute-start.4 = (bf16[2,64,1024]{2,1,0:T(8,128)(2,1)S(1)}, bf16[2,64,1024]{2,1,0:T(8,128)(2,1)S(1)}, u32[]{:S(2)}, u32[]{:S(2)}) collective-permute-start(bf16[2,64,1024]{2,1,0:T(8,128)(2,1)S(1)} %maximum_select_fusion.1.refs_0_), channel_id=1, source_target_pairs={{0,14},{1,15},{2,0},{3,1},{4,2},{5,3},{6,4},{7,5},{8,6},{9,7},{10,... | collective-permute-start | bytes 786440 | tf_op jit(solution)/shard_map/ppermute | solution.py:29
  11.3 5.9 %collective-permute-done.4.refs_4_ = bf16[2,64,1024]{2,1,0:T(8,128)(2,1)S(1)} collective-permute-done((bf16[2,64,1024]{2,1,0:T(8,128)(2,1)S(1)}, bf16[2,64,1024]{2,1,0:T(8,128)(2,1)S(1)}, u32[]{:S(2)}, u32[]{:S(2)}) %collective-permute-start.4) | collective-permute-done | bytes 262176 | tf_op jit(solution)/shard_map/ppermute | solution.py:29
  17.1 3.7 %collective-permute-start.5 = (bf16[2,64,1024]{2,1,0:T(8,128)(2,1)S(1)}, bf16[2,64,1024]{2,1,0:T(8,128)(2,1)}, u32[]{:S(2)}, u32[]{:S(2)}) collective-permute-start(bf16[2,64,1024]{2,1,0:T(8,128)(2,1)S(1)} %collective-permute-done.4.refs_4_), channel_id=1, source_target_pairs={{0,14},{1,15},{2,0},{3,1},{4,2},{5,3},{6,4},{7,5},{8,6},{9,7},{10,... | collective-permute-start | bytes 786440 | tf_op jit(solution)/shard_map/ppermute | solution.py:29
  21.5 4.3 %collective-permute-done.5.refs_5_ = bf16[2,64,1024]{2,1,0:T(8,128)(2,1)} collective-permute-done((bf16[2,64,1024]{2,1,0:T(8,128)(2,1)S(1)}, bf16[2,64,1024]{2,1,0:T(8,128)(2,1)}, u32[]{:S(2)}, u32[]{:S(2)}) %collective-permute-start.5) | collective-permute-done | bytes 262176 | tf_op jit(solution)/shard_map/ppermute | solution.py:29
  25.8 3.8 %collective-permute-start.6 = (bf16[2,64,1024]{2,1,0:T(8,128)(2,1)}, bf16[2,64,1024]{2,1,0:T(8,128)(2,1)S(1)}, u32[]{:S(2)}, u32[]{:S(2)}) collective-permute-start(bf16[2,64,1024]{2,1,0:T(8,128)(2,1)} %collective-permute-done.5.refs_5_), channel_id=1, source_target_pairs={{0,14},{1,15},{2,0},{3,1},{4,2},{5,3},{6,4},{7,5},{8,6},{9,7},{10,... | collective-permute-start | bytes 786440 | tf_op jit(solution)/shard_map/ppermute | solution.py:29
  29.9 4.2 %collective-permute-done.6.refs_6_ = bf16[2,64,1024]{2,1,0:T(8,128)(2,1)S(1)} collective-permute-done((bf16[2,64,1024]{2,1,0:T(8,128)(2,1)}, bf16[2,64,1024]{2,1,0:T(8,128)(2,1)S(1)}, u32[]{:S(2)}, u32[]{:S(2)}) %collective-permute-start.6) | collective-permute-done | bytes 262176 | tf_op jit(solution)/shard_map/ppermute | solution.py:29
  34.1 3.7 %collective-permute-start.22 = (bf16[2,32,1024]{2,1,0:T(8,128)(2,1)S(1)}, bf16[2,32,1024]{2,1,0:T(8,128)(2,1)S(1)}, u32[]{:S(2)}, u32[]{:S(2)}) collective-permute-start(bf16[2,32,1024]{2,1,0:T(8,128)(2,1)S(1)} %slice.105), channel_id=1, source_target_pairs={{0,14},{1,15},{2,0},{3,1},{4,2},{5,3},{6,4},{7,5},{8,6},{9,7},{10,... | collective-permute-start | bytes 393224 | tf_op jit(solution)/shard_map/ppermute | solution.py:29
  37.8 2.5 %collective-permute-done.22.refs_7_ = bf16[2,32,1024]{2,1,0:T(8,128)(2,1)S(1)} collective-permute-done((bf16[2,32,1024]{2,1,0:T(8,128)(2,1)S(1)}, bf16[2,32,1024]{2,1,0:T(8,128)(2,1)S(1)}, u32[]{:S(2)}, u32[]{:S(2)}) %collective-permute-start.22) | collective-permute-done | bytes 131104 | tf_op jit(solution)/shard_map/ppermute | solution.py:29
  45.7 5.9 %shard_map.89 = (bf16[4,32,2048]{2,1,0:T(8,128)(2,1)}, bf16[4,32,2048]{2,1,0:T(8,128)(2,1)}, bf16[4,32,2048]{2,1,0:T(8,128)(2,1)}, f32[4,32,2048]{2,1,0:T(8,128)S(1)}) custom-call(s32[16]{0:T(128)S(1)} %get-tuple-element.88.table, bf16[2,64,1024]{2,1,0:T(8,128)(2,1)S(1)} %maximum_select_fusion.1.refs_0_, bf16[2,64,1024]{2,1,0:T(8,128)(2,1)S(1)} %copy-done.18, ...), custom_call_target="tpu_custom_call" | custom-call | flops 2147483648 | bytes 8781824 | tf_op jit(solution)/shard_map/pallas_call | solution.py:72
  53.9 2.9 %collective-permute-start.24 = (bf16[4,32,2048]{2,1,0:T(8,128)(2,1)}, bf16[4,32,2048]{2,1,0:T(8,128)(2,1)S(1)}, u32[]{:S(2)}, u32[]{:S(2)}) collective-permute-start(bf16[4,32,2048]{2,1,0:T(8,128)(2,1)} %get-tuple-element.69), channel_id=1, source_target_pairs={{0,128},{1,33},{2,130},{3,35},{4,132},{5,37},{6,134},{7,39},{8,136... | collective-permute-start | bytes 1572872 | tf_op jit(solution)/shard_map/ppermute | solution.py:29
  63.0 6.9 %collective-permute-done.24.p2 = bf16[4,32,2048]{2,1,0:T(8,128)(2,1)S(1)} collective-permute-done((bf16[4,32,2048]{2,1,0:T(8,128)(2,1)}, bf16[4,32,2048]{2,1,0:T(8,128)(2,1)S(1)}, u32[]{:S(2)}, u32[]{:S(2)}) %collective-permute-start.24) | collective-permute-done | bytes 524320 | tf_op jit(solution)/shard_map/ppermute | solution.py:29
  76.8 5.8 %shard_map.85 = (bf16[4,32,2048]{2,1,0:T(8,128)(2,1)}, bf16[4,32,2048]{2,1,0:T(8,128)(2,1)}, bf16[4,32,2048]{2,1,0:T(8,128)(2,1)}, f32[4,32,2048]{2,1,0:T(8,128)S(1)}) custom-call(s32[16]{0:T(128)S(1)} %broadcast_select_fusion.3.table, bf16[2,64,1024]{2,1,0:T(8,128)(2,1)S(1)} %maximum_select_fusion.1.refs_0_, bf16[2,64,1024]{2,1,0:T(8,128)(2,1)S(1)} %copy-done.19, ...), custom_call_target="tpu_custom_call" | custom-call | flops 2147483648 | bytes 8781824 | tf_op jit(solution)/shard_map/pallas_call | solution.py:72
  82.6 3.3 %collective-permute-start.10 = (bf16[4,32,2048]{2,1,0:T(8,128)(2,1)}, bf16[4,32,2048]{2,1,0:T(8,128)(2,1)S(1)}, u32[]{:S(2)}, u32[]{:S(2)}) collective-permute-start(bf16[4,32,2048]{2,1,0:T(8,128)(2,1)} %get-tuple-element.58), channel_id=1, source_target_pairs={{0,32},{1,129},{2,34},{3,131},{4,36},{5,133},{6,38},{7,135},{8,40}... | collective-permute-start | bytes 1572872 | tf_op jit(solution)/shard_map/ppermute | solution.py:29
  94.0 2.9 %collective-permute-done.29 = bf16[32,2048]{1,0:T(8,128)(2,1)} collective-permute-done((bf16[32,2048]{1,0:T(8,128)(2,1)S(1)}, bf16[32,2048]{1,0:T(8,128)(2,1)}, u32[]{:S(2)}, u32[]{:S(2)}) %collective-permute-start.29) | collective-permute-done | bytes 131104 | tf_op jit(solution)/shard_map/ppermute | solution.py:29
  98.4 3.5 %collective-permute-done.31 = bf16[32,2048]{1,0:T(8,128)(2,1)} collective-permute-done((bf16[32,2048]{1,0:T(8,128)(2,1)S(1)}, bf16[32,2048]{1,0:T(8,128)(2,1)}, u32[]{:S(2)}, u32[]{:S(2)}) %collective-permute-start.31) | collective-permute-done | bytes 131104 | tf_op jit(solution)/shard_map/ppermute | solution.py:29
  105.5 3.3 %collective-permute-start.13 = (bf16[32,2048]{1,0:T(8,128)(2,1)S(1)}, bf16[32,2048]{1,0:T(8,128)(2,1)S(1)}, u32[]{:S(2)}, u32[]{:S(2)}) collective-permute-start(bf16[32,2048]{1,0:T(8,128)(2,1)S(1)} %get-tuple-element.62), channel_id=1, source_target_pairs={{0,128},{1,33},{2,130},{3,35},{4,132},{5,37},{6,134},{7,39},{8,136... | collective-permute-start | bytes 393224 | tf_op jit(solution)/shard_map/ppermute | solution.py:29
  108.8 2.9 %collective-permute-done.12.q1 = bf16[32,2048]{1,0:T(8,128)(2,1)S(1)} collective-permute-done((bf16[32,2048]{1,0:T(8,128)(2,1)S(1)}, bf16[32,2048]{1,0:T(8,128)(2,1)S(1)}, u32[]{:S(2)}, u32[]{:S(2)}) %collective-permute-start.12) | collective-permute-done | bytes 131104 | tf_op jit(solution)/shard_map/ppermute | solution.py:29
  119.7 2.8 %collective-permute-start.33 = (bf16[4,32,2048]{2,1,0:T(8,128)(2,1)S(1)}, bf16[4,32,2048]{2,1,0:T(8,128)(2,1)S(1)}, u32[]{:S(2)}, u32[]{:S(2)}) collective-permute-start(bf16[4,32,2048]{2,1,0:T(8,128)(2,1)S(1)} %pad_maximum_fusion.1.refs_4_), channel_id=1, source_target_pairs={{0,32},{1,129},{2,34},{3,131},{4,36},{5,133},{6,38},{7,135},{8,40}... | collective-permute-start | bytes 1572872 | tf_op jit(solution)/shard_map/ppermute | solution.py:29
  123.4 3.5 %collective-permute-done.17 = bf16[32,2048]{1,0:T(8,128)(2,1)S(1)} collective-permute-done((bf16[32,2048]{1,0:T(8,128)(2,1)S(1)}, bf16[32,2048]{1,0:T(8,128)(2,1)S(1)}, u32[]{:S(2)}, u32[]{:S(2)}) %collective-permute-start.17) | collective-permute-done | bytes 131104 | tf_op jit(solution)/shard_map/ppermute | solution.py:29
  127.0 2.9 %collective-permute-start.20 = (bf16[4,32,2048]{2,1,0:T(8,128)(2,1)S(1)}, bf16[4,32,2048]{2,1,0:T(8,128)(2,1)S(1)}, u32[]{:S(2)}, u32[]{:S(2)}) collective-permute-start(bf16[4,32,2048]{2,1,0:T(8,128)(2,1)S(1)} %pad_maximum_fusion.refs_0_), channel_id=1, source_target_pairs={{0,128},{1,33},{2,130},{3,35},{4,132},{5,37},{6,134},{7,39},{8,136... | collective-permute-start | bytes 1572872 | tf_op jit(solution)/shard_map/ppermute | solution.py:29
  130.4 7.7 %collective-permute-done.33.refs_6_ = bf16[4,32,2048]{2,1,0:T(8,128)(2,1)S(1)} collective-permute-done((bf16[4,32,2048]{2,1,0:T(8,128)(2,1)S(1)}, bf16[4,32,2048]{2,1,0:T(8,128)(2,1)S(1)}, u32[]{:S(2)}, u32[]{:S(2)}) %collective-permute-start.33) | collective-permute-done | bytes 524320 | tf_op jit(solution)/shard_map/ppermute | solution.py:29
  138.1 9.8 %collective-permute-done.34.refs_7_ = bf16[4,32,2048]{2,1,0:T(8,128)(2,1)S(1)} collective-permute-done((bf16[4,32,2048]{2,1,0:T(8,128)(2,1)S(1)}, bf16[4,32,2048]{2,1,0:T(8,128)(2,1)S(1)}, u32[]{:S(2)}, u32[]{:S(2)}) %collective-permute-start.34) | collective-permute-done | bytes 524320 | tf_op jit(solution)/shard_map/ppermute | solution.py:29
  147.9 6.0 %shard_map.92 = (f32[4,2,32,1024]{3,2,1,0:T(8,128)S(1)}, f32[6,2,32,1024]{3,2,1,0:T(8,128)S(1)}, f32[6,2,32,1024]{3,2,1,0:T(8,128)S(1)}) custom-call(s32[32]{0:T(128)S(1)} %pad_add_fusion.table, bf16[4,32,2048]{2,1,0:T(8,128)(2,1)S(1)} %pad_maximum_fusion.refs_0_, bf16[4,32,2048]{2,1,0:T(8,128)(2,1)S(1)} %collective-permute-done.19.refs_1_, ...), custom_call_target="tpu_custom_call" | custom-call | flops 4294967296 | bytes 12582912 | tf_op jit(solution)/shard_map/pallas_call | solution.py:72
  154.1 3.4 %collective-permute-start.39 = (bf16[2,32,1024]{2,1,0:T(8,128)(2,1)S(1)}, bf16[2,32,1024]{2,1,0:T(8,128)(2,1)S(1)}, u32[]{:S(2)}, u32[]{:S(2)}) collective-permute-start(bf16[2,32,1024]{2,1,0:T(8,128)(2,1)S(1)} %get-tuple-element.96), channel_id=1, source_target_pairs={{0,14},{1,15},{2,0},{3,1},{4,2},{5,3},{6,4},{7,5},{8,6},{9,7},{10,... | collective-permute-start | bytes 393224 | tf_op jit(solution)/shard_map/ppermute | solution.py:29
  157.5 3.5 %collective-permute-done.35 = bf16[2,32,1024]{2,1,0:T(8,128)(2,1)S(1)} collective-permute-done((bf16[2,32,1024]{2,1,0:T(8,128)(2,1)S(1)}, bf16[2,32,1024]{2,1,0:T(8,128)(2,1)S(1)}, u32[]{:S(2)}, u32[]{:S(2)}) %collective-permute-start.35) | collective-permute-done | bytes 131104 | tf_op jit(solution)/shard_map/ppermute | solution.py:29
  161.2 3.3 %collective-permute-start.40 = (bf16[2,2,32,1024]{3,2,1,0:T(8,128)(2,1)S(1)}, bf16[2,2,32,1024]{3,2,1,0:T(8,128)(2,1)S(1)}, u32[]{:S(2)}, u32[]{:S(2)}) collective-permute-start(bf16[2,2,32,1024]{3,2,1,0:T(8,128)(2,1)S(1)} %fusion.3), channel_id=1, source_target_pairs={{0,14},{1,15},{2,0},{3,1},{4,2},{5,3},{6,4},{7,5},{8,6},{9,7},{10,... | collective-permute-start | bytes 786440 | tf_op jit(solution)/shard_map/ppermute | solution.py:29
  164.5 5.4 %collective-permute-done.36 = bf16[2,2,32,1024]{3,2,1,0:T(8,128)(2,1)S(1)} collective-permute-done((bf16[2,2,32,1024]{3,2,1,0:T(8,128)(2,1)S(1)}, bf16[2,2,32,1024]{3,2,1,0:T(8,128)(2,1)S(1)}, u32[]{:S(2)}, u32[]{:S(2)}) %collective-permute-start.36) | collective-permute-done | bytes 262176 | tf_op jit(solution)/shard_map/ppermute | solution.py:29
  170.2 3.3 %collective-permute-start.41 = (bf16[2,2,32,1024]{3,2,1,0:T(8,128)(2,1)S(1)}, bf16[2,2,32,1024]{3,2,1,0:T(8,128)(2,1)S(1)}, u32[]{:S(2)}, u32[]{:S(2)}) collective-permute-start(bf16[2,2,32,1024]{3,2,1,0:T(8,128)(2,1)S(1)} %add_convert_fusion.1), channel_id=1, source_target_pairs={{0,14},{1,15},{2,0},{3,1},{4,2},{5,3},{6,4},{7,5},{8,6},{9,7},{10,... | collective-permute-start | bytes 786440 | tf_op jit(solution)/shard_map/ppermute | solution.py:29
  173.5 4.6 %collective-permute-done.37 = bf16[2,2,32,1024]{3,2,1,0:T(8,128)(2,1)S(1)} collective-permute-done((bf16[2,2,32,1024]{3,2,1,0:T(8,128)(2,1)S(1)}, bf16[2,2,32,1024]{3,2,1,0:T(8,128)(2,1)S(1)}, u32[]{:S(2)}, u32[]{:S(2)}) %collective-permute-start.37) | collective-permute-done | bytes 262176 | tf_op jit(solution)/shard_map/ppermute | solution.py:29
  178.4 3.3 %collective-permute-start.42 = (bf16[2,2,32,1024]{3,2,1,0:T(8,128)(2,1)S(1)}, bf16[2,2,32,1024]{3,2,1,0:T(8,128)(2,1)S(1)}, u32[]{:S(2)}, u32[]{:S(2)}) collective-permute-start(bf16[2,2,32,1024]{3,2,1,0:T(8,128)(2,1)S(1)} %add_convert_fusion), channel_id=1, source_target_pairs={{0,14},{1,15},{2,0},{3,1},{4,2},{5,3},{6,4},{7,5},{8,6},{9,7},{10,... | collective-permute-start | bytes 786440 | tf_op jit(solution)/shard_map/ppermute | solution.py:29
  181.8 4.1 %collective-permute-done.38 = bf16[2,2,32,1024]{3,2,1,0:T(8,128)(2,1)S(1)} collective-permute-done((bf16[2,2,32,1024]{3,2,1,0:T(8,128)(2,1)S(1)}, bf16[2,2,32,1024]{3,2,1,0:T(8,128)(2,1)S(1)}, u32[]{:S(2)}, u32[]{:S(2)}) %collective-permute-start.38) | collective-permute-done | bytes 262176 | tf_op jit(solution)/shard_map/ppermute | solution.py:29
  (138 shorter events, 50.2 us)
Async XLA Ops:
  0.6 39.6 %collective-permute-start.8 = (bf16[1024,1024]{1,0:T(8,128)(2,1)}, bf16[1024,1024]{1,0:T(8,128)(2,1)S(1)}, u32[]{:S(2)}, u32[]{:S(2)}) collective-permute-start(bf16[1024,1024]{1,0:T(8,128)(2,1)} %refs_8_.5), channel_id=1, source_target_pairs={{0,1},{1,0},{2,3},{3,2},{4,5},{5,4},{6,7},{7,6},{8,9},{9,8},{10,11... | collective-permute-start | bytes 6291464 | tf_op jit(solution)/shard_map/ppermute | solution.py:29
  5.3 11.8 %collective-permute-start.4 = (bf16[2,64,1024]{2,1,0:T(8,128)(2,1)S(1)}, bf16[2,64,1024]{2,1,0:T(8,128)(2,1)S(1)}, u32[]{:S(2)}, u32[]{:S(2)}) collective-permute-start(bf16[2,64,1024]{2,1,0:T(8,128)(2,1)S(1)} %maximum_select_fusion.1.refs_0_), channel_id=1, source_target_pairs={{0,14},{1,15},{2,0},{3,1},{4,2},{5,3},{6,4},{7,5},{8,6},{9,7},{10,... | collective-permute-start | bytes 786440 | tf_op jit(solution)/shard_map/ppermute | solution.py:29
  11.2 9.6 %collective-permute-start.1 = (bf16[2,64,1024]{2,1,0:T(8,128)(2,1)S(1)}, bf16[2,64,1024]{2,1,0:T(8,128)(2,1)S(1)}, u32[]{:S(2)}, u32[]{:S(2)}) collective-permute-start(bf16[2,64,1024]{2,1,0:T(8,128)(2,1)S(1)} %maximum_select_fusion.1.refs_0_), channel_id=1, source_target_pairs={{0,2},{1,3},{2,4},{3,5},{4,6},{5,7},{6,8},{7,9},{8,10},{9,11},{10,... | collective-permute-start | bytes 786440 | tf_op jit(solution)/shard_map/ppermute | solution.py:29
  17.1 8.7 %collective-permute-start.5 = (bf16[2,64,1024]{2,1,0:T(8,128)(2,1)S(1)}, bf16[2,64,1024]{2,1,0:T(8,128)(2,1)}, u32[]{:S(2)}, u32[]{:S(2)}) collective-permute-start(bf16[2,64,1024]{2,1,0:T(8,128)(2,1)S(1)} %collective-permute-done.4.refs_4_), channel_id=1, source_target_pairs={{0,14},{1,15},{2,0},{3,1},{4,2},{5,3},{6,4},{7,5},{8,6},{9,7},{10,... | collective-permute-start | bytes 786440 | tf_op jit(solution)/shard_map/ppermute | solution.py:29
  20.8 9.0 %collective-permute-start.2 = (bf16[2,64,1024]{2,1,0:T(8,128)(2,1)S(1)}, bf16[2,64,1024]{2,1,0:T(8,128)(2,1)}, u32[]{:S(2)}, u32[]{:S(2)}) collective-permute-start(bf16[2,64,1024]{2,1,0:T(8,128)(2,1)S(1)} %collective-permute-done.1.refs_1_), channel_id=1, source_target_pairs={{0,2},{1,3},{2,4},{3,5},{4,6},{5,7},{6,8},{7,9},{8,10},{9,11},{10,... | collective-permute-start | bytes 786440 | tf_op jit(solution)/shard_map/ppermute | solution.py:29
  25.8 8.3 %collective-permute-start.6 = (bf16[2,64,1024]{2,1,0:T(8,128)(2,1)}, bf16[2,64,1024]{2,1,0:T(8,128)(2,1)S(1)}, u32[]{:S(2)}, u32[]{:S(2)}) collective-permute-start(bf16[2,64,1024]{2,1,0:T(8,128)(2,1)} %collective-permute-done.5.refs_5_), channel_id=1, source_target_pairs={{0,14},{1,15},{2,0},{3,1},{4,2},{5,3},{6,4},{7,5},{8,6},{9,7},{10,... | collective-permute-start | bytes 786440 | tf_op jit(solution)/shard_map/ppermute | solution.py:29
  29.8 8.0 %collective-permute-start.3 = (bf16[2,64,1024]{2,1,0:T(8,128)(2,1)}, bf16[2,64,1024]{2,1,0:T(8,128)(2,1)S(1)}, u32[]{:S(2)}, u32[]{:S(2)}) collective-permute-start(bf16[2,64,1024]{2,1,0:T(8,128)(2,1)} %collective-permute-done.2.refs_2_), channel_id=1, source_target_pairs={{0,2},{1,3},{2,4},{3,5},{4,6},{5,7},{6,8},{7,9},{8,10},{9,11},{10,... | collective-permute-start | bytes 786440 | tf_op jit(solution)/shard_map/ppermute | solution.py:29
  52.4 10.6 %collective-permute-start.23 = (bf16[4,32,2048]{2,1,0:T(8,128)(2,1)}, bf16[4,32,2048]{2,1,0:T(8,128)(2,1)S(1)}, u32[]{:S(2)}, u32[]{:S(2)}) collective-permute-start(bf16[4,32,2048]{2,1,0:T(8,128)(2,1)} %get-tuple-element.68), channel_id=1, source_target_pairs={{0,64},{1,17},{2,66},{3,19},{4,68},{5,21},{6,70},{7,23},{8,72},{9,... | collective-permute-start | bytes 1572872 | tf_op jit(solution)/shard_map/ppermute | solution.py:29
  53.9 15.9 %collective-permute-start.24 = (bf16[4,32,2048]{2,1,0:T(8,128)(2,1)}, bf16[4,32,2048]{2,1,0:T(8,128)(2,1)S(1)}, u32[]{:S(2)}, u32[]{:S(2)}) collective-permute-start(bf16[4,32,2048]{2,1,0:T(8,128)(2,1)} %get-tuple-element.69), channel_id=1, source_target_pairs={{0,128},{1,33},{2,130},{3,35},{4,132},{5,37},{6,134},{7,39},{8,136... | collective-permute-start | bytes 1572872 | tf_op jit(solution)/shard_map/ppermute | solution.py:29
  56.8 13.0 %collective-permute-start.25 = (bf16[4,32,2048]{2,1,0:T(8,128)(2,1)}, bf16[4,32,2048]{2,1,0:T(8,128)(2,1)}, u32[]{:S(2)}, u32[]{:S(2)}) collective-permute-start(bf16[4,32,2048]{2,1,0:T(8,128)(2,1)} %get-tuple-element.70), channel_id=1, source_target_pairs={{0,192},{1,49},{2,194},{3,51},{4,196},{5,53},{6,198},{7,55},{8,200... | collective-permute-start | bytes 1572872 | tf_op jit(solution)/shard_map/ppermute | solution.py:29
  59.3 26.5 %collective-permute-start.15 = (f32[2,64,1024]{2,1,0:T(8,128)}, f32[2,64,1024]{2,1,0:T(8,128)S(1)}, u32[]{:S(2)}, u32[]{:S(2)}) collective-permute-start(f32[2,64,1024]{2,1,0:T(8,128)} %get-tuple-element.65), channel_id=1, source_target_pairs={{0,1},{1,0},{2,3},{3,2},{4,5},{5,4},{6,7},{7,6},{8,9},{9,8},{10,11... | collective-permute-start | bytes 1572872 | tf_op jit(solution)/shard_map/ppermute | solution.py:29
  60.4 13.8 %collective-permute-start.7 = (bf16[2,32,1024]{2,1,0:T(8,128)(2,1)S(1)}, bf16[2,32,1024]{2,1,0:T(8,128)(2,1)S(1)}, u32[]{:S(2)}, u32[]{:S(2)}) collective-permute-start(bf16[2,32,1024]{2,1,0:T(8,128)(2,1)S(1)} %slice.104), channel_id=1, source_target_pairs={{0,2},{1,3},{2,4},{3,5},{4,6},{5,7},{6,8},{7,9},{8,10},{9,11},{10,... | collective-permute-start | bytes 393224 | tf_op jit(solution)/shard_map/ppermute | solution.py:29
  71.2 15.5 %collective-permute-start.26 = (bf16[32,2048]{1,0:T(8,128)(2,1)S(1)}, bf16[32,2048]{1,0:T(8,128)(2,1)S(1)}, u32[]{:S(2)}, u32[]{:S(2)}) collective-permute-start(bf16[32,2048]{1,0:T(8,128)(2,1)S(1)} %get-tuple-element.72), channel_id=1, source_target_pairs={{0,16},{1,65},{2,18},{3,67},{4,20},{5,69},{6,22},{7,71},{8,24},{9,... | collective-permute-start | bytes 393224 | tf_op jit(solution)/shard_map/ppermute | solution.py:29
  71.8 17.3 %collective-permute-start.27 = (bf16[32,2048]{1,0:T(8,128)(2,1)S(1)}, bf16[32,2048]{1,0:T(8,128)(2,1)S(1)}, u32[]{:S(2)}, u32[]{:S(2)}) collective-permute-start(bf16[32,2048]{1,0:T(8,128)(2,1)S(1)} %get-tuple-element.73), channel_id=1, source_target_pairs={{0,32},{1,129},{2,34},{3,131},{4,36},{5,133},{6,38},{7,135},{8,40}... | collective-permute-start | bytes 393224 | tf_op jit(solution)/shard_map/ppermute | solution.py:29
  74.2 14.9 %collective-permute-start.28 = (bf16[32,2048]{1,0:T(8,128)(2,1)S(1)}, bf16[32,2048]{1,0:T(8,128)(2,1)S(1)}, u32[]{:S(2)}, u32[]{:S(2)}) collective-permute-start(bf16[32,2048]{1,0:T(8,128)(2,1)S(1)} %get-tuple-element.74), channel_id=1, source_target_pairs={{0,48},{1,193},{2,50},{3,195},{4,52},{5,197},{6,54},{7,199},{8,56}... | collective-permute-start | bytes 393224 | tf_op jit(solution)/shard_map/ppermute | solution.py:29
  82.6 21.2 %collective-permute-start.10 = (bf16[4,32,2048]{2,1,0:T(8,128)(2,1)}, bf16[4,32,2048]{2,1,0:T(8,128)(2,1)S(1)}, u32[]{:S(2)}, u32[]{:S(2)}) collective-permute-start(bf16[4,32,2048]{2,1,0:T(8,128)(2,1)} %get-tuple-element.58), channel_id=1, source_target_pairs={{0,32},{1,129},{2,34},{3,131},{4,36},{5,133},{6,38},{7,135},{8,40}... | collective-permute-start | bytes 1572872 | tf_op jit(solution)/shard_map/ppermute | solution.py:29
  85.8 18.0 %collective-permute-start.11 = (bf16[4,32,2048]{2,1,0:T(8,128)(2,1)}, bf16[4,32,2048]{2,1,0:T(8,128)(2,1)S(1)}, u32[]{:S(2)}, u32[]{:S(2)}) collective-permute-start(bf16[4,32,2048]{2,1,0:T(8,128)(2,1)} %get-tuple-element.59), channel_id=1, source_target_pairs={{0,48},{1,193},{2,50},{3,195},{4,52},{5,197},{6,54},{7,199},{8,56}... | collective-permute-start | bytes 1572872 | tf_op jit(solution)/shard_map/ppermute | solution.py:29
  86.7 17.1 %collective-permute-start.9 = (bf16[4,32,2048]{2,1,0:T(8,128)(2,1)}, bf16[4,32,2048]{2,1,0:T(8,128)(2,1)}, u32[]{:S(2)}, u32[]{:S(2)}) collective-permute-start(bf16[4,32,2048]{2,1,0:T(8,128)(2,1)} %get-tuple-element.57), channel_id=1, source_target_pairs={{0,16},{1,65},{2,18},{3,67},{4,20},{5,69},{6,22},{7,71},{8,24},{9,... | collective-permute-start | bytes 1572872 | tf_op jit(solution)/shard_map/ppermute | solution.py:29
  103.0 26.9 %collective-permute-start.32 = (bf16[4,32,2048]{2,1,0:T(8,128)(2,1)S(1)}, bf16[4,32,2048]{2,1,0:T(8,128)(2,1)S(1)}, u32[]{:S(2)}, u32[]{:S(2)}) collective-permute-start(bf16[4,32,2048]{2,1,0:T(8,128)(2,1)S(1)} %pad_maximum_fusion.1.refs_4_), channel_id=1, source_target_pairs={{0,16},{1,65},{2,18},{3,67},{4,20},{5,69},{6,22},{7,71},{8,24},{9,... | collective-permute-start | bytes 1572872 | tf_op jit(solution)/shard_map/ppermute | solution.py:29
  105.5 7.6 %collective-permute-start.13 = (bf16[32,2048]{1,0:T(8,128)(2,1)S(1)}, bf16[32,2048]{1,0:T(8,128)(2,1)S(1)}, u32[]{:S(2)}, u32[]{:S(2)}) collective-permute-start(bf16[32,2048]{1,0:T(8,128)(2,1)S(1)} %get-tuple-element.62), channel_id=1, source_target_pairs={{0,128},{1,33},{2,130},{3,35},{4,132},{5,37},{6,134},{7,39},{8,136... | collective-permute-start | bytes 393224 | tf_op jit(solution)/shard_map/ppermute | solution.py:29
  119.0 7.9 %collective-permute-start.17 = (bf16[32,2048]{1,0:T(8,128)(2,1)S(1)}, bf16[32,2048]{1,0:T(8,128)(2,1)S(1)}, u32[]{:S(2)}, u32[]{:S(2)}) collective-permute-start(bf16[32,2048]{1,0:T(8,128)(2,1)S(1)} %get-tuple-element.66), channel_id=1, source_target_pairs={{0,32},{1,129},{2,34},{3,131},{4,36},{5,133},{6,38},{7,135},{8,40}... | collective-permute-start | bytes 393224 | tf_op jit(solution)/shard_map/ppermute | solution.py:29
  119.7 18.4 %collective-permute-start.33 = (bf16[4,32,2048]{2,1,0:T(8,128)(2,1)S(1)}, bf16[4,32,2048]{2,1,0:T(8,128)(2,1)S(1)}, u32[]{:S(2)}, u32[]{:S(2)}) collective-permute-start(bf16[4,32,2048]{2,1,0:T(8,128)(2,1)S(1)} %pad_maximum_fusion.1.refs_4_), channel_id=1, source_target_pairs={{0,32},{1,129},{2,34},{3,131},{4,36},{5,133},{6,38},{7,135},{8,40}... | collective-permute-start | bytes 1572872 | tf_op jit(solution)/shard_map/ppermute | solution.py:29
  122.5 25.4 %collective-permute-start.34 = (bf16[4,32,2048]{2,1,0:T(8,128)(2,1)S(1)}, bf16[4,32,2048]{2,1,0:T(8,128)(2,1)S(1)}, u32[]{:S(2)}, u32[]{:S(2)}) collective-permute-start(bf16[4,32,2048]{2,1,0:T(8,128)(2,1)S(1)} %pad_maximum_fusion.1.refs_4_), channel_id=1, source_target_pairs={{0,48},{1,193},{2,50},{3,195},{4,52},{5,197},{6,54},{7,199},{8,56}... | collective-permute-start | bytes 1572872 | tf_op jit(solution)/shard_map/ppermute | solution.py:29
  127.0 20.9 %collective-permute-start.19 = (bf16[4,32,2048]{2,1,0:T(8,128)(2,1)S(1)}, bf16[4,32,2048]{2,1,0:T(8,128)(2,1)S(1)}, u32[]{:S(2)}, u32[]{:S(2)}) collective-permute-start(bf16[4,32,2048]{2,1,0:T(8,128)(2,1)S(1)} %pad_maximum_fusion.refs_0_), channel_id=1, source_target_pairs={{0,64},{1,17},{2,66},{3,19},{4,68},{5,21},{6,70},{7,23},{8,72},{9,... | collective-permute-start | bytes 1572872 | tf_op jit(solution)/shard_map/ppermute | solution.py:29
  127.0 20.9 %collective-permute-start.20 = (bf16[4,32,2048]{2,1,0:T(8,128)(2,1)S(1)}, bf16[4,32,2048]{2,1,0:T(8,128)(2,1)S(1)}, u32[]{:S(2)}, u32[]{:S(2)}) collective-permute-start(bf16[4,32,2048]{2,1,0:T(8,128)(2,1)S(1)} %pad_maximum_fusion.refs_0_), channel_id=1, source_target_pairs={{0,128},{1,33},{2,130},{3,35},{4,132},{5,37},{6,134},{7,39},{8,136... | collective-permute-start | bytes 1572872 | tf_op jit(solution)/shard_map/ppermute | solution.py:29
  130.0 17.9 %collective-permute-start.21 = (bf16[4,32,2048]{2,1,0:T(8,128)(2,1)S(1)}, bf16[4,32,2048]{2,1,0:T(8,128)(2,1)S(1)}, u32[]{:S(2)}, u32[]{:S(2)}) collective-permute-start(bf16[4,32,2048]{2,1,0:T(8,128)(2,1)S(1)} %pad_maximum_fusion.refs_0_), channel_id=1, source_target_pairs={{0,192},{1,49},{2,194},{3,51},{4,196},{5,53},{6,198},{7,55},{8,200... | collective-permute-start | bytes 1572872 | tf_op jit(solution)/shard_map/ppermute | solution.py:29
  161.1 8.9 %collective-permute-start.36 = (bf16[2,2,32,1024]{3,2,1,0:T(8,128)(2,1)S(1)}, bf16[2,2,32,1024]{3,2,1,0:T(8,128)(2,1)S(1)}, u32[]{:S(2)}, u32[]{:S(2)}) collective-permute-start(bf16[2,2,32,1024]{3,2,1,0:T(8,128)(2,1)S(1)} %fusion.2), channel_id=1, source_target_pairs={{0,2},{1,3},{2,4},{3,5},{4,6},{5,7},{6,8},{7,9},{8,10},{9,11},{10,... | collective-permute-start | bytes 786440 | tf_op jit(solution)/shard_map/ppermute | solution.py:29
  161.2 8.9 %collective-permute-start.40 = (bf16[2,2,32,1024]{3,2,1,0:T(8,128)(2,1)S(1)}, bf16[2,2,32,1024]{3,2,1,0:T(8,128)(2,1)S(1)}, u32[]{:S(2)}, u32[]{:S(2)}) collective-permute-start(bf16[2,2,32,1024]{3,2,1,0:T(8,128)(2,1)S(1)} %fusion.3), channel_id=1, source_target_pairs={{0,14},{1,15},{2,0},{3,1},{4,2},{5,3},{6,4},{7,5},{8,6},{9,7},{10,... | collective-permute-start | bytes 786440 | tf_op jit(solution)/shard_map/ppermute | solution.py:29
  170.1 8.1 %collective-permute-start.37 = (bf16[2,2,32,1024]{3,2,1,0:T(8,128)(2,1)S(1)}, bf16[2,2,32,1024]{3,2,1,0:T(8,128)(2,1)S(1)}, u32[]{:S(2)}, u32[]{:S(2)}) collective-permute-start(bf16[2,2,32,1024]{3,2,1,0:T(8,128)(2,1)S(1)} %add_convert_fusion.3), channel_id=1, source_target_pairs={{0,2},{1,3},{2,4},{3,5},{4,6},{5,7},{6,8},{7,9},{8,10},{9,11},{10,... | collective-permute-start | bytes 786440 | tf_op jit(solution)/shard_map/ppermute | solution.py:29
  170.2 8.0 %collective-permute-start.41 = (bf16[2,2,32,1024]{3,2,1,0:T(8,128)(2,1)S(1)}, bf16[2,2,32,1024]{3,2,1,0:T(8,128)(2,1)S(1)}, u32[]{:S(2)}, u32[]{:S(2)}) collective-permute-start(bf16[2,2,32,1024]{3,2,1,0:T(8,128)(2,1)S(1)} %add_convert_fusion.1), channel_id=1, source_target_pairs={{0,14},{1,15},{2,0},{3,1},{4,2},{5,3},{6,4},{7,5},{8,6},{9,7},{10,... | collective-permute-start | bytes 786440 | tf_op jit(solution)/shard_map/ppermute | solution.py:29
  178.2 7.7 %collective-permute-start.38 = (bf16[2,2,32,1024]{3,2,1,0:T(8,128)(2,1)S(1)}, bf16[2,2,32,1024]{3,2,1,0:T(8,128)(2,1)S(1)}, u32[]{:S(2)}, u32[]{:S(2)}) collective-permute-start(bf16[2,2,32,1024]{3,2,1,0:T(8,128)(2,1)S(1)} %add_convert_fusion.2), channel_id=1, source_target_pairs={{0,2},{1,3},{2,4},{3,5},{4,6},{5,7},{6,8},{7,9},{8,10},{9,11},{10,... | collective-permute-start | bytes 786440 | tf_op jit(solution)/shard_map/ppermute | solution.py:29
  178.4 7.5 %collective-permute-start.42 = (bf16[2,2,32,1024]{3,2,1,0:T(8,128)(2,1)S(1)}, bf16[2,2,32,1024]{3,2,1,0:T(8,128)(2,1)S(1)}, u32[]{:S(2)}, u32[]{:S(2)}) collective-permute-start(bf16[2,2,32,1024]{3,2,1,0:T(8,128)(2,1)S(1)} %add_convert_fusion), channel_id=1, source_target_pairs={{0,14},{1,15},{2,0},{3,1},{4,2},{5,3},{6,4},{7,5},{8,6},{9,7},{10,... | collective-permute-start | bytes 786440 | tf_op jit(solution)/shard_map/ppermute | solution.py:29
  (34 other events, 319.3 us)
